TPU v7x, 32 devices: a whole 2x2x4 slice. The times are simulated.
32 devices in a mesh: row: 8 (over z, y), col: 4 (over x, core).
Axes of the slice: x: 2, y: 2, z: 4, core: 2. Of those that a mesh axis runs over, the one named last changes fastest.
Arguments:
- rhs: float32 [65536, 256], P(('row', 'col')), may hold values from -6 to 6
- block_target: int32 [512], P(('row', 'col')), may hold values from 0 to 127, as said below
- pivot_inverse: float32 [32768, 1024], P(('row', 'col')), may hold values from -0.25 to 3, as said below
- update_factor: float32 [32768, 1024], P(('row', 'col')), may hold values from -0.1875 to 0.1875
- root_inverse: float32 [4096, 4096], P('row', 'col'), may hold values from -0.25 to 3, as said below
- update_map: int32 [256], P(('row', 'col')), may hold values from 0 to 31
Outputs:
- front_solution: float32 [32768, 256], P(('row', 'col'))
- root_solution: float32 [4096, 256], P(('row', 'col'))
Inputs may be any that keep to these rules, and one draw needn't show every extreme that they name: block_target[g] is e * 16 + s: block g goes to the device of row index e in its own column, slot s there. Each device sends exactly 2 blocks to each of 8 devices of its column and none to the others; every slot of every device is filled exactly once. `pivot_inverse`: each device's block of 1024 rows is lower triangular with its diagonal positive. `root_inverse`: lower triangular with its diagonal positive.
All inputs are finite; a program needn't handle non-finite values.
Results may differ from a plain program's by a relative error of at most 0.000073.
Values sent between devices are 32-bit elements; how exact they have to be, the bound alone decides.
A program may use at most 192 MiB of HBM per device.

v0:
```python
import functools
import jax
import jax.numpy as jnp
from jax import lax
from jax.experimental import pallas as pl
from jax.experimental.pallas import tpu as pltpu
from jax.sharding import PartitionSpec as P

BLK = 128
CAP = 2
PARTS = 2
CHUNKS = 16
CORE_SKEW = 2
LEAD = 6
SKEW = 4
MESH = pl.DeviceIdType.MESH
VMEM = pl.BlockSpec(memory_space=pltpu.VMEM)
SMEM = pl.BlockSpec(memory_space=pltpu.SMEM)
ANY = pl.BlockSpec(memory_space=pl.ANY)


def split(value):
    high = value.astype(jnp.bfloat16)
    low = (value - high.astype(jnp.float32)).astype(jnp.bfloat16)
    return high, low


def dot3(a, b_high, b_low):
    a_high, a_low = split(a)
    total = jnp.dot(a_high, b_low, preferred_element_type=jnp.float32)
    total += jnp.dot(a_low, b_high, preferred_element_type=jnp.float32)
    return total + jnp.dot(a_high, b_high, preferred_element_type=jnp.float32)


def forward_kernel(
    n_row, n_col, order, target_ref, map_ref, rhs_ref, pivot_hbm, factor_hbm, inverse_hbm,
    solved, out,
    staging, messages, arrived_a, arrived_b, slots, slots_smem, place_ref, weights, high, low, updated,
    give, got_core, got_x, y_up, y_down, y_ds, mid, z_up, z_down, z_ds, product, got_col,
    weight_sem, slot_sem, send, recv, send_int, recv_int,
    core_send, core_recv, x_send, x_recv, y_send, y_recv, z_send, z_recv, col_send, col_recv,
):
    n_y = max(1, n_col // 2)
    n_z, n_x = n_row // n_y, n_col // 2
    r, c = lax.axis_index("row"), lax.axis_index("col")
    z, y, x, k = r // n_y, r % n_y, c // 2, c % 2
    size = n_row * BLK
    step_rows = size // CHUNKS
    held = rhs_ref.shape[0]
    rows = solved.shape[0]
    half = rows // BLK
    tile = 2 * BLK
    base = got_core.at[0]
    arrived = (arrived_a, arrived_b)
    lanes = solved.shape[1] // PARTS

    def cols(h):
        return pl.ds(h * lanes, lanes)


    def remote(src, dst, ss, rs, device):
        return pltpu.make_async_remote_copy(
            src_ref=src, dst_ref=dst, send_sem=ss, recv_sem=rs, device_id=device, device_id_type=MESH
        )

    barrier = pltpu.get_barrier_semaphore()
    for d in order:
        pl.semaphore_signal(barrier, inc=1, device_id=(r ^ d, c), device_id_type=MESH)
    for d in range(1, n_col):
        pl.semaphore_signal(barrier, inc=1, device_id=(r, (c + d) % n_col), device_id_type=MESH)

    pivot_copy = pltpu.make_async_copy(pivot_hbm, weights.at[pl.ds(0, rows)], weight_sem.at[0])
    factor_copy = pltpu.make_async_copy(factor_hbm, weights.at[pl.ds(rows, rows)], weight_sem.at[1])
    pivot_copy.start()
    factor_copy.start()

    lane = lax.broadcasted_iota(jnp.int32, (8, 128), 1)
    targets = [target_ref[g] for g in range(held)]

    def chosen(peer):
        first, last = jnp.int32(held), jnp.int32(-1)
        slot_first, slot_last = jnp.int32(-1), jnp.int32(-1)
        for g in range(held):
            match = lax.div(targets[g], held) == peer
            fresh = jnp.logical_and(match, last < 0)
            first = jnp.where(fresh, g, first)
            slot_first = jnp.where(fresh, lax.rem(targets[g], held), slot_first)
            last = jnp.where(match, g, last)
            slot_last = jnp.where(match, lax.rem(targets[g], held), slot_last)
        message = jnp.where(lane == 0, slot_first, slot_last)
        return jnp.minimum(first, held - 1), jnp.maximum(last, 0), message

    def data_copy(n, d, h):
        return remote(
            staging.at[n, :, :, cols(h)],
            arrived[h].at[pl.ds(r * CAP, CAP)],
            send.at[h, n],
            recv.at[h, n],
            (r ^ d, c),
        )

    def slot_copy(n, d):
        return remote(messages.at[n], slots.at[r], send_int.at[n], recv_int.at[n], (r ^ d, c))

    picks = []
    for n, d in enumerate(order):
        first, last, messages[n] = chosen(r ^ d)
        picks.append((first, last))
        staging[n, 0] = rhs_ref[first]
        staging[n, 1] = rhs_ref[last]
        if n == 0:
            pl.semaphore_wait(barrier, n_row + n_col - 2)
        slot_copy(n, d).start()
        data_copy(n, d, 0).start()
    for h in range(1, PARTS):
        for n, d in enumerate(order):
            data_copy(n, d, h).start()
    first, last, slots[r] = chosen(r)
    for h in range(PARTS):
        arrived[h][r * CAP] = rhs_ref[first, :, cols(h)]
        arrived[h][r * CAP + 1] = rhs_ref[last, :, cols(h)]

    for n, d in enumerate(order):
        slot_copy(n, d).wait_recv()
    to_smem = pltpu.make_async_copy(slots, slots_smem, slot_sem)
    to_smem.start()
    to_smem.wait()
    found = [slots_smem[s, 0, rank] for s in range(n_row) for rank in range(CAP)]
    for b in range(held):
        place = jnp.int32(0)
        for j, slot in enumerate(found):
            place = jnp.where(slot == b, j, place)
        place_ref[b] = place

    pivot_copy.wait()
    factor_copy.wait()
    def front(h):
        for n, d in enumerate(order):
            data_copy(n, d, h).wait_recv()
        for b in range(half):
            part = pl.ds(b * BLK, BLK)
            high[part, cols(h)], low[part, cols(h)] = split(arrived[h][place_ref[b]])
        for start in range(0, rows, tile):
            deep = start + tile
            solved[start : start + tile, cols(h)] = dot3(
                weights[start : start + tile, :deep], high[:deep, cols(h)], low[:deep, cols(h)]
            )
        for start in range(0, rows, tile):
            part = pl.ds(start, tile)
            high[part, cols(h)], low[part, cols(h)] = split(solved[part, cols(h)])
        for start in range(0, rows, tile):
            value = dot3(
                weights[rows + start : rows + start + tile], high[:rows, cols(h)], low[:rows, cols(h)]
            )
            for step in range(tile // BLK):
                b = start // BLK + step
                updated[b, :, cols(h)] = (
                    arrived[h][place_ref[half + b]] - value[step * BLK : (step + 1) * BLK]
                )

    deep = min(rows, size)
    inverse_copies = [
        pltpu.make_async_copy(
            inverse_hbm.at[:, pl.ds(n * deep, deep)],
            weights.at[pl.ds(n * n_col * BLK, n_col * BLK), pl.ds(0, deep)],
            weight_sem.at[n],
        )
        for n in range(size // deep)
    ]
    def rows_of(i):
        return pl.ds(pl.multiple_of(i * step_rows, step_rows), step_rows)

    per_block = BLK // step_rows
    maps = [map_ref[b] for b in range(half)]

    partner = (r, c - k + (1 - k))

    def root(h):
        def dense(column, i):
            block = column * n_row + i // per_block
            part = pl.ds(pl.multiple_of((i % per_block) * step_rows, step_rows), step_rows)
            value = None
            for b in range(half):
                term = updated[b, part, cols(h)] * jnp.where(maps[b] == block, 1.0, 0.0)
                value = term if value is None else value + term
            return value

        def core_copy(d, i):
            return remote(
                give.at[d, rows_of(i), cols(h)], got_core.at[d, rows_of(i), cols(h)], core_send.at[h, d], core_recv.at[h, d, i], partner
            )

        def x_copy(d, i):
            return remote(
                got_core.at[d, rows_of(i), cols(h)],
                got_x.at[d - 1, rows_of(i), cols(h)],
                x_send.at[h, d - 1],
                x_recv.at[h, d - 1, i],
                (r, ((x + d) % n_x) * 2 + k),
            )

        def stage_core(i):
            for d in range(n_x - 1, -1, -1):
                give[d, rows_of(i), cols(h)] = dense(2 * ((x + d) % n_x) + (1 - k), i)
                core_copy(d, i).start()

        def stage_x(i):
            for d in range(n_x - 1, -1, -1):
                value = dense(2 * ((x + d) % n_x) + k, i)
                core_copy(d, i).wait_recv()
                got_core[d, rows_of(i), cols(h)] = value + got_core[d, rows_of(i), cols(h)]
                if d:
                    x_copy(d, i).start()

        def join_x(i):
            value = base[rows_of(i), cols(h)]
            for d in range(1, n_x):
                x_copy(d, i).wait_recv()
                value = value + got_x[d - 1, rows_of(i), cols(h)]
            base[rows_of(i), cols(h)] = value

        def line(n, pos, stride, own, up, down, ds, ss, rs):
            def send_up(i, source):
                return remote(source.at[rows_of(i), cols(h)], up.at[rows_of(i), cols(h)], ss.at[h, 0], rs.at[h, 0, i], (r + stride, c))

            def send_down(i, source):
                return remote(source.at[rows_of(i), cols(h)], down.at[rows_of(i), cols(h)], ss.at[h, 1], rs.at[h, 1, i], (r - stride, c))

            def hop(step, i):
                for place, landed, total, go in (
                    (pos, up, up, send_up),
                    (n - 1 - pos, down, ds, send_down),
                ):
                    @pl.when(place == step)
                    def _():
                        if step == 0:
                            go(i, own).start()
                        else:
                            go(i, total).wait_recv()
                            if step < n - 1:
                                total[rows_of(i), cols(h)] = own[rows_of(i), cols(h)] + landed[rows_of(i), cols(h)]
                                go(i, total).start()

            def total(i, write):
                part = rows_of(i)

                @pl.when(pos == 0)
                def _():
                    write(part, own[part, cols(h)] + down[part, cols(h)])

                @pl.when(pos == n - 1)
                def _():
                    write(part, own[part, cols(h)] + up[part, cols(h)])

                if n > 2:
                    @pl.when(jnp.logical_and(pos > 0, pos < n - 1))
                    def _():
                        write(part, up[part, cols(h)] + down[part, cols(h)])

            def drain():
                whole = pl.ds(0, size)

                @pl.when(pos < n - 1)
                def _():
                    remote(own.at[whole, cols(h)], up.at[whole, cols(h)], ss.at[h, 0], rs.at[h, 0, 0], (r + stride, c)).wait_send()

                @pl.when(pos > 0)
                def _():
                    remote(own.at[whole, cols(h)], down.at[whole, cols(h)], ss.at[h, 1], rs.at[h, 1, 0], (r - stride, c)).wait_send()

            return hop, total, drain

        y_hop, y_total, y_drain = line(n_y, y, 1, base, y_up, y_down, y_ds, y_send, y_recv)
        z_hop, z_total, z_drain = line(n_z, z, n_y, mid, z_up, z_down, z_ds, z_send, z_recv)

        def write_mid(part, value):
            mid[part, cols(h)] = value

        def write_split(part, value):
            high[part, cols(h)], low[part, cols(h)] = split(value)

        def y_first(i):
            join_x(i)
            y_hop(0, i)

        def z_first(i):
            y_hop(n_y - 1, i)
            y_total(i, write_mid)
            z_hop(0, i)

        def z_last(i):
            z_hop(n_z - 1, i)
            z_total(i, write_split)

        def drain():
            for d in range(n_x):
                remote(
                    give.at[d, :, cols(h)], got_core.at[d, :, cols(h)],
                    core_send.at[h, d], core_recv.at[h, d, 0], partner,
                ).wait_send()
            for d in range(1, n_x):
                remote(
                    got_core.at[d, :, cols(h)], got_x.at[d - 1, :, cols(h)],
                    x_send.at[h, d - 1], x_recv.at[h, d - 1, 0],
                    (r, ((x + d) % n_x) * 2 + k),
                ).wait_send()
            y_drain()
            z_drain()

        at = CORE_SKEW + LEAD
        head = [(0, stage_core), (CORE_SKEW, stage_x), (at, y_first)]
        for step in range(1, n_y - 1):
            at += SKEW
            head.append((at, functools.partial(y_hop, step)))
        head.append((at + SKEW, z_first))
        tail = [((step - 1) * SKEW, functools.partial(z_hop, step)) for step in range(1, n_z - 1)]
        tail.append(((n_z - 2) * SKEW, z_last))
        return head, tail, drain

    def run(stages):
        @pl.loop(0, CHUNKS + max(offset for offset, _ in stages))
        def _(t):
            for offset, stage in stages:
                i = t - offset

                @pl.when(jnp.logical_and(i >= 0, i < CHUNKS))
                def _():
                    stage(i)

    parts = [root(h) for h in range(PARTS)]
    left = []
    for h, (head, tail, _) in enumerate(parts):
        front(h)
        if h == PARTS - 1:
            for copy in inverse_copies:
                copy.start()
            after = max(offset for offset, _ in head) + SKEW
            tail = [(after + offset, stage) for offset, stage in tail]
            run(left + head + tail)
        else:
            run(left + head)
            left = tail

    for copy in inverse_copies:
        copy.wait()
    for start in range(0, n_col * BLK, tile):
        value = None
        for n in range(size // deep):
            part = slice(n * deep, (n + 1) * deep)
            at_row = n * n_col * BLK + start
            term = dot3(weights[at_row : at_row + tile, :deep], high[part], low[part])
            value = term if value is None else value + term
        product[start : start + tile] = value

    def col_copy(d):
        to = (c + d) % n_col
        return remote(
            product.at[pl.ds(pl.multiple_of(to * BLK, BLK), BLK)],
            got_col.at[d - 1],
            col_send.at[d - 1],
            col_recv.at[d - 1],
            (r, to),
        )

    for d in range(1, n_col):
        col_copy(d).start()
    value = product[pl.ds(pl.multiple_of(c * BLK, BLK), BLK)]
    for d in range(1, n_col):
        col_copy(d).wait_recv()
        value = value + got_col[d - 1]
    out[...] = value

    for n, d in enumerate(order):
        slot_copy(n, d).wait_send()
        for h in range(PARTS):
            data_copy(n, d, h).wait_send()
    for d in range(1, n_col):
        col_copy(d).wait_send()
    for _, _, drain in parts:
        drain()


def shards(rhs, block_target, pivot_inverse, update_factor, root_inverse, update_map):
    n_row, n_col = lax.axis_size("row"), lax.axis_size("col")
    n_x = n_col // 2
    width = rhs.shape[1]
    held = rhs.shape[0] // BLK
    rows = pivot_inverse.shape[0]
    size = n_row * BLK
    f32 = jnp.float32
    half = n_row // 2
    near = list(range(half - 1, 1, -1))
    cross = list(range(n_row - 1, half - 1, -1))
    order = []
    for n in range(max(len(near), len(cross))):
        order += near[n : n + 1] + cross[n : n + 1]
    order += [1]
    slab = pltpu.VMEM((size, width), f32)
    longest = max(rows, size)
    dma = pltpu.SemaphoreType.DMA
    return pl.pallas_call(
        functools.partial(forward_kernel, n_row, n_col, order),
        out_shape=(
            jax.ShapeDtypeStruct((rows, width), f32),
            jax.ShapeDtypeStruct((BLK, width), f32),
        ),
        in_specs=[SMEM, SMEM, VMEM, ANY, ANY, ANY],
        out_specs=(VMEM, VMEM),
        scratch_shapes=[
            pltpu.VMEM((n_row - 1, CAP, BLK, width), f32),
            pltpu.VMEM((n_row - 1, 8, 128), jnp.int32),
            pltpu.VMEM((n_row * CAP, BLK, width // PARTS), f32),
            pltpu.VMEM((n_row * CAP, BLK, width // PARTS), f32),
            pltpu.VMEM((n_row, 8, 128), jnp.int32),
            pltpu.SMEM((n_row, 8, 128), jnp.int32),
            pltpu.SMEM((held,), jnp.int32),
            pltpu.VMEM((2 * rows, rows), f32),
            pltpu.VMEM((longest, width), jnp.bfloat16),
            pltpu.VMEM((longest, width), jnp.bfloat16),
            pltpu.VMEM((rows // BLK, BLK, width), f32),
            pltpu.VMEM((n_x, size, width), f32),
            pltpu.VMEM((n_x, size, width), f32),
            pltpu.VMEM((n_x - 1, size, width), f32),
        ]
        + [slab] * 7
        + [
            pltpu.VMEM((n_col * BLK, width), f32),
            pltpu.VMEM((n_col - 1, BLK, width), f32),
            dma((2,)),
            dma(()),
        ]
        + [dma((PARTS, n_row - 1))] * 2
        + [dma((n_row - 1,))] * 2
        + [
            dma((PARTS, n_x)),
            dma((PARTS, n_x, CHUNKS)),
            dma((PARTS, n_x - 1)),
            dma((PARTS, n_x - 1, CHUNKS)),
            dma((PARTS, 2)),
            dma((PARTS, 2, CHUNKS)),
            dma((PARTS, 2)),
            dma((PARTS, 2, CHUNKS)),
            dma((n_col - 1,)),
            dma((n_col - 1,)),
        ],
        compiler_params=pltpu.CompilerParams(
            collective_id=0, has_side_effects=True, vmem_limit_bytes=67043328
        ),
        name="forward",
    )(block_target, update_map, rhs.reshape(held, BLK, width), pivot_inverse, update_factor, root_inverse)


def solution(mesh):
    return jax.shard_map(
        shards,
        mesh=mesh,
        in_specs=(
            P(("row", "col"), None),
            P(("row", "col")),
            P(("row", "col"), None),
            P(("row", "col"), None),
            P("row", "col"),
            P(("row", "col")),
        ),
        out_specs=(P(("row", "col"), None), P(("row", "col"), None)),
        check_vma=False,
    )
```

profile of v0, /device:TPU:0, one launch (start us, length us, event | category | flops | bytes accessed | tf_op | source)
XLA Modules:
  0.0 108.9 jit_solution(12651599896767453615)
XLA Ops:
  0.6 104.4 %forward.1 = (f32[1024,256]{1,0:T(8,128)}, f32[128,256]{1,0:T(8,128)}) custom-call(s32[16]{0:T(128)} %target_ref.1, s32[8]{0:T(128)} %map_ref.1, f32[16,128,256]{2,1,0:T(8,128)} %bitcast.1, f32[1024,1024]{1,0:T(8,128)} %pivot_hbm.1, f32[1024,1024]{1,0:T(8,128)} %factor_hbm.1, f32[512,1024]{1,0:T(8,128)} %inverse_hbm.1), custom_call_target="tpu_custom_call" | custom-call | tf_op jit(solution)/shard_map/forward/pallas_call | solution.py:401
  105.1 2.3 %copy.10 = f32[1024,256]{1,0:T(8,128)} copy(f32[1024,256]{1,0:T(8,128)} %get-tuple-element.4) | data formatting | bytes 2097152
  107.4 1.6 %copy.11 = f32[128,256]{1,0:T(8,128)} copy(f32[128,256]{1,0:T(8,128)} %get-tuple-element.5) | data formatting | bytes 262144
where the time goes:
time: 110 us; the launch traced here: 109 us
  Pallas kernels  104 us (95%)
  local copies, waits for them, and re-layouts  3.83 us (3%)
    pallas_call x1, Pallas kernels, shards(): pl.pallas_call(functools.partial(forward_kernel, n_row, n_col, order), ou...  104 us
    unnamed x2, local copies, waits for them, and re-layouts  3.83 us

commit v1 on v0

v1 whole, which is shorter than its diff:
```python
import functools
import jax
import jax.numpy as jnp
from jax import lax
from jax.experimental import pallas as pl
from jax.experimental.pallas import tpu as pltpu
from jax.sharding import PartitionSpec as P

BLK = 128
CAP = 2
LANES = 128
HALF_LANES = 64
TILE = 256
EARLY_ROWS = 64
LAST_ROWS = 32
CORE_SKEW = 2
LEAD = 4
SKEW = 3
Z_SKEW = 4
MESH = pl.DeviceIdType.MESH
VMEM = pl.BlockSpec(memory_space=pltpu.VMEM)
SMEM = pl.BlockSpec(memory_space=pltpu.SMEM)
ANY = pl.BlockSpec(memory_space=pl.ANY)


def split(value):
    high = value.astype(jnp.bfloat16)
    low = (value - high.astype(jnp.float32)).astype(jnp.bfloat16)
    return high, low


def dot3(a_high, a_low, b_high, b_low):
    total = jnp.dot(a_high, b_low, preferred_element_type=jnp.float32)
    total += jnp.dot(a_low, b_high, preferred_element_type=jnp.float32)
    return total + jnp.dot(a_high, b_high, preferred_element_type=jnp.float32)


def run(stages):
    @pl.loop(0, max(offset + count for offset, count, _ in stages))
    def _(t):
        for offset, count, stage in stages:
            i = t - offset

            @pl.when(jnp.logical_and(i >= 0, i < count))
            def _():
                stage(i)


def forward_kernel(
    n_row, n_col, order, target_ref, map_ref, rhs_ref, pivot_hbm, factor_hbm, inverse_hbm,
    solved, out,
    staging, messages, slots, slots_smem, place_ref, weights,
    p_high, p_low, w_high, w_low, x_high, x_low, updated,
    give, got_core, got_x, got_y, mid, up, down, ds, total, got_all, product, got_col,
    weight_sem, slot_sem, send, recv, send_int, recv_int,
    core_send, core_recv, x_send, x_recv, y_send, y_recv, z_send, z_recv, all_send, all_recv,
    col_send, col_recv, *arrived,
):
    n_y = max(1, n_col // 2)
    n_z, n_x = n_row // n_y, n_col // 2
    r, c = lax.axis_index("row"), lax.axis_index("col")
    z, y, x, k = r // n_y, r % n_y, c // 2, c % 2
    held = rhs_ref.shape[0]
    rows = solved.shape[0]
    half = rows // BLK
    parts = len(arrived)
    last = parts - 1
    per_seg = n_row // n_y
    seg = per_seg // 2 * BLK
    out_rows = n_col * BLK
    pair = BLK // 2

    chunk = [LAST_ROWS if q == last else EARLY_ROWS for q in range(parts)]
    steps = [seg // rows_ for rows_ in chunk]

    side = jnp.where(lax.broadcasted_iota(jnp.int32, (1, LANES), 1) < HALF_LANES, 0, 1)

    def swap(value):
        return pltpu.roll(value, HALF_LANES, 1)

    def remote(src, dst, ss, rs, device):
        return pltpu.make_async_remote_copy(
            src_ref=src, dst_ref=dst, send_sem=ss, recv_sem=rs, device_id=device, device_id_type=MESH
        )

    barrier = pltpu.get_barrier_semaphore()
    for d in order:
        pl.semaphore_signal(barrier, inc=1, device_id=(r ^ d, c), device_id_type=MESH)
    for d in range(1, n_col):
        pl.semaphore_signal(barrier, inc=1, device_id=(r, (c + d) % n_col), device_id_type=MESH)

    pivot_copy = pltpu.make_async_copy(pivot_hbm, weights.at[pl.ds(0, rows)], weight_sem.at[0])
    factor_copy = pltpu.make_async_copy(factor_hbm, weights.at[pl.ds(rows, rows)], weight_sem.at[1])
    pivot_copy.start()
    factor_copy.start()

    lane = lax.broadcasted_iota(jnp.int32, (8, 128), 1)
    targets = [target_ref[g] for g in range(held)]

    def chosen(peer):
        first, last_ = jnp.int32(held), jnp.int32(-1)
        slot_first, slot_last = jnp.int32(-1), jnp.int32(-1)
        for g in range(held):
            match = lax.div(targets[g], held) == peer
            fresh = jnp.logical_and(match, last_ < 0)
            first = jnp.where(fresh, g, first)
            slot_first = jnp.where(fresh, lax.rem(targets[g], held), slot_first)
            last_ = jnp.where(match, g, last_)
            slot_last = jnp.where(match, lax.rem(targets[g], held), slot_last)
        message = jnp.where(lane == 0, slot_first, slot_last)
        return jnp.minimum(first, held - 1), jnp.maximum(last_, 0), message

    def stage(first, second, tile):
        cols = slice(tile * LANES, (tile + 1) * LANES)
        a, b = rhs_ref[first, :, cols], rhs_ref[second, :, cols]
        return jnp.where(side == 0, a, swap(b)), jnp.where(side == 0, swap(a), b)

    def data_copy(n, d, q):
        return remote(staging.at[q, n], arrived[q].at[r], send.at[q, n], recv.at[q, n], (r ^ d, c))

    def slot_copy(n, d):
        return remote(messages.at[n], slots.at[r], send_int.at[n], recv_int.at[n], (r ^ d, c))

    picks = []
    for n, d in enumerate(order):
        first, second, messages[n] = chosen(r ^ d)
        picks.append((first, second))
        staging[0, n], staging[1, n] = stage(first, second, 0)
        if n == 0:
            pl.semaphore_wait(barrier, n_row + n_col - 2)
        slot_copy(n, d).start()
        data_copy(n, d, 0).start()
    for n, d in enumerate(order):
        data_copy(n, d, 1).start()
    for tile in range(1, parts // 2):
        for n, d in enumerate(order):
            staging[2 * tile, n], staging[2 * tile + 1, n] = stage(*picks[n], tile)
        for q in (2 * tile, 2 * tile + 1):
            for n, d in enumerate(order):
                data_copy(n, d, q).start()
    first, second, slots[r] = chosen(r)
    for tile in range(parts // 2):
        arrived[2 * tile][r], arrived[2 * tile + 1][r] = stage(first, second, tile)

    pivot_copy.wait()
    factor_copy.wait()
    for start in range(0, rows, TILE):
        band = slice(start, start + TILE)
        p_high[band], p_low[band] = split(weights[band])
    for start in range(0, rows, TILE):
        band = slice(start, start + TILE)
        u_high, u_low = split(weights[rows + start : rows + start + TILE])
        for at in range(0, rows, TILE):
            cols = slice(at, at + TILE)
            w_high[band, cols], w_low[band, cols] = split(
                dot3(u_high[:, at:], u_low[:, at:], p_high[at:, cols], p_low[at:, cols])
            )

    inverse_at = []
    inverse_copies = []
    bands = rows // (2 * seg)
    for e in range(n_y):
        at = (e // bands * out_rows, e % bands * 2 * seg)
        inverse_at.append(at)
        inverse_copies.append(
            pltpu.make_async_copy(
                inverse_hbm.at[:, pl.ds(pl.multiple_of((y - e + n_y) % n_y * (2 * seg), 2 * seg), 2 * seg)],
                weights.at[pl.ds(at[0], out_rows), pl.ds(at[1], 2 * seg)],
                weight_sem.at[e],
            )
        )
    for copy in inverse_copies:
        copy.start()

    for n, d in enumerate(order):
        slot_copy(n, d).wait_recv()
    to_smem = pltpu.make_async_copy(slots, slots_smem, slot_sem)
    to_smem.start()
    to_smem.wait()
    found = [slots_smem[s, 0, rank] for s in range(n_row) for rank in range(CAP)]
    for b in range(held):
        place = jnp.int32(0)
        for j, slot in enumerate(found):
            place = jnp.where(slot == b, j, place)
        place_ref[b] = place

    maps = [map_ref[b] for b in range(half)]
    partner = (r, c - k + (1 - k))

    def twice(q, b):
        place = place_ref[b]
        value = arrived[q][lax.div(place, CAP)]
        return jnp.where(side == lax.rem(place, CAP), value, swap(value))

    def update(q):
        for n, d in enumerate(order):
            data_copy(n, d, q).wait_recv()
        for b in range(half):
            part = slice(b * BLK, (b + 1) * BLK)
            x_high[part], x_low[part] = split(twice(q, b))
        for start in range(0, rows, TILE):
            band = slice(start, start + TILE)
            value = dot3(w_high[band], w_low[band], x_high[...], x_low[...])
            for step in range(TILE // BLK):
                b = start // BLK + step
                updated[b] = twice(q, half + b) - value[step * BLK : (step + 1) * BLK]

    def solve(q):
        for b in range(half):
            part = slice(b * BLK, (b + 1) * BLK)
            x_high[part], x_low[part] = split(jnp.where(side == 0, twice(q, b), twice(q + 1, b)))
        for start in range(0, rows, TILE):
            band, deep = slice(start, start + TILE), slice(0, start + TILE)
            solved[band, q // 2 * LANES : (q // 2 + 1) * LANES] = dot3(
                p_high[band, deep], p_low[band, deep], x_high[deep], x_low[deep]
            )

    def within(q, i):
        return pl.ds(pl.multiple_of(i * chunk[q], chunk[q]), chunk[q])

    def wide(q, i):
        return pl.ds(pl.multiple_of(i * (n_y * chunk[q]), n_y * chunk[q]), n_y * chunk[q])

    def place_of(q, i):
        return pl.ds(pl.multiple_of(q * seg + i * chunk[q], chunk[q]), chunk[q])

    def dense(q, column, i, e):
        at = i * chunk[q]
        block = column * n_row + (y + e) % n_y * per_seg + at // BLK
        wanted = block + side * (per_seg // 2)
        part = pl.ds(pl.multiple_of(at % BLK, chunk[q]), chunk[q])
        value = None
        for b in range(half):
            term = jnp.where(wanted == maps[b], updated[b, part], 0.0)
            value = term if value is None else value + term
        return value

    def core_copy(q, d, part, i):
        return remote(
            give.at[q, d, part], got_core.at[q, d, part], core_send.at[q, d], core_recv.at[q, d, i], partner
        )

    def x_copy(q, d, part, i):
        return remote(
            got_core.at[q, d, part], got_x.at[q, d - 1, part], x_send.at[q, d - 1], x_recv.at[q, d - 1, i],
            (r, (x + d) % n_x * 2 + k),
        )

    def y_device(e):
        return (r - y + (y + e) % n_y, c)

    def slab(q, i, e):
        return pl.ds(pl.multiple_of((i * n_y + e) * chunk[q], chunk[q]), chunk[q])

    def y_copy(q, e, i):
        return remote(
            got_core.at[q, 0, slab(q, i, e)], got_y.at[q, e - 1, within(q, i)],
            y_send.at[q, e - 1], y_recv.at[q, e - 1, i], y_device(e),
        )

    def all_copy(q, e, i):
        return remote(
            total.at[place_of(q, i)], got_all.at[q, e - 1, within(q, i)],
            all_send.at[q, e - 1], all_recv.at[q, e - 1, i], y_device(e),
        )

    def up_copy(q, i, source):
        part = place_of(q, i)
        return remote(source.at[part], up.at[part], z_send.at[q, 0], z_recv.at[q, 0, i], (r + n_y, c))

    def down_copy(q, i, source):
        part = place_of(q, i)
        return remote(source.at[part], down.at[part], z_send.at[q, 1], z_recv.at[q, 1, i], (r - n_y, c))

    def stage_core(q, i):
        for d in range(n_x - 1, -1, -1):
            for e in range(n_y - 1, -1, -1):
                give[q, d, slab(q, i, e)] = dense(q, 2 * ((x + d) % n_x) + (1 - k), i, e)
            core_copy(q, d, wide(q, i), i).start()

    def stage_x(q, i):
        for d in range(n_x - 1, -1, -1):
            values = [dense(q, 2 * ((x + d) % n_x) + k, i, e) for e in range(n_y)]
            core_copy(q, d, wide(q, i), i).wait_recv()
            for e in range(n_y):
                part = slab(q, i, e)
                got_core[q, d, part] = values[e] + got_core[q, d, part]
            if d:
                x_copy(q, d, wide(q, i), i).start()

    def stage_y(q, i):
        for d in range(1, n_x):
            x_copy(q, d, wide(q, i), i).wait_recv()
        for e in range(n_y - 1, -1, -1):
            part = slab(q, i, e)
            value = got_core[q, 0, part]
            for d in range(1, n_x):
                value = value + got_x[q, d - 1, part]
            if e:
                got_core[q, 0, part] = value
                y_copy(q, e, i).start()
            else:
                mid[place_of(q, i)] = value

    def hop(step, q, i):
        part = place_of(q, i)
        for at, landed, summed, go in ((z, up, up, up_copy), (n_z - 1 - z, down, ds, down_copy)):
            @pl.when(at == step)
            def _():
                if step == 0:
                    go(q, i, mid).start()
                else:
                    go(q, i, summed).wait_recv()
                    if step < n_z - 1:
                        summed[part] = mid[part] + landed[part]
                        go(q, i, summed).start()

    def z_first(q, i):
        part = place_of(q, i)
        value = mid[part]
        for e in range(1, n_y):
            y_copy(q, e, i).wait_recv()
            value = value + got_y[q, e - 1, within(q, i)]
        mid[part] = value
        hop(0, q, i)

    def z_last(q, i):
        hop(n_z - 1, q, i)
        part = place_of(q, i)

        @pl.when(z == 0)
        def _():
            total[part] = mid[part] + down[part]

        @pl.when(z == n_z - 1)
        def _():
            total[part] = mid[part] + up[part]

        if n_z > 2:
            @pl.when(jnp.logical_and(z > 0, z < n_z - 1))
            def _():
                total[part] = up[part] + down[part]

        for e in range(1, n_y):
            all_copy(q, e, i).start()

    def multiply(q):
        left = [None] * (out_rows // TILE)
        right = [None] * (out_rows // TILE)
        for e in range(n_y):
            if e:
                for i in range(steps[q]):
                    all_copy(q, e, i).wait_recv()
            b_high, b_low = split(got_all[q, e - 1] if e else total[q * seg : (q + 1) * seg])
            at_row, at_col = inverse_at[e]
            for n in range(out_rows // TILE):
                band = slice(at_row + n * TILE, at_row + (n + 1) * TILE)
                for sums, start in ((left, at_col), (right, at_col + seg)):
                    term = dot3(*split(weights[band, start : start + seg]), b_high, b_low)
                    sums[n] = term if sums[n] is None else sums[n] + term
        for n in range(out_rows // TILE):
            value = jnp.where(side == 0, left[n], right[n])
            value = value + swap(value)
            for step in range(TILE // BLK):
                top = value[step * BLK : step * BLK + pair]
                bottom = value[step * BLK + pair : (step + 1) * BLK]
                product[q, n * (TILE // BLK) + step] = jnp.where(side == 0, top, bottom)
        for d in range(1, n_col):
            col_copy(q, d).start()

    def col_copy(q, d):
        to = (c + d) % n_col
        return remote(product.at[q, to], got_col.at[q, d - 1], col_send.at[q, d - 1], col_recv.at[q, d - 1], (r, to))

    def collect(q):
        sums = []
        for part in (q, q + 1):
            value = product[part, c]
            for d in range(1, n_col):
                col_copy(part, d).wait_recv()
                value = value + got_col[part, d - 1]
            sums.append(value)
        cols = slice(q // 2 * LANES, (q // 2 + 1) * LANES)
        out[:pair, cols] = jnp.where(side == 0, sums[0], swap(sums[1]))
        out[pair:, cols] = jnp.where(side == 0, swap(sums[0]), sums[1])

    def of(fn, *args):
        return functools.partial(fn, *args)

    for q in range(last):
        update(q)
        stages = [
            (0, steps[q], of(stage_core, q)),
            (1, steps[q], of(stage_x, q)),
            (3, steps[q], of(stage_y, q)),
        ]
        if q:
            stages.append((0, steps[q - 1], of(z_first, q - 1)))
        run(stages)
        if q % 2:
            solve(q - 1)

    for copy in inverse_copies:
        copy.wait()
    update(last)
    at = CORE_SKEW + LEAD + SKEW
    stages = [
        (0, steps[last], of(stage_core, last)),
        (CORE_SKEW, steps[last], of(stage_x, last)),
        (CORE_SKEW + LEAD, steps[last], of(stage_y, last)),
        (at, steps[last], of(z_first, last)),
        (0, steps[last - 1], of(z_first, last - 1)),
        (2, 1, lambda i: solve(last - 1)),
    ]
    for step in range(1, n_z - 1):
        stages.append((at + step * SKEW, steps[last], of(hop, step, last)))
    stages.append((at + (n_z - 1) * SKEW, steps[last], of(z_last, last)))
    for q in range(last):
        begin = sum(steps[:q])
        for step in range(1, n_z - 1):
            stages.append((begin + (step - 1) * Z_SKEW, steps[q], of(hop, step, q)))
        stages.append((begin + (n_z - 2) * Z_SKEW, steps[q], of(z_last, q)))
    run(stages)
    for q in range(parts):
        multiply(q)
    for q in range(0, parts, 2):
        collect(q)

    for n, d in enumerate(order):
        slot_copy(n, d).wait_send()
        for q in range(parts):
            data_copy(n, d, q).wait_send()
    for q in range(parts):
        for d in range(1, n_col):
            col_copy(q, d).wait_send()
        everything = pl.ds(0, n_y * seg)
        for d in range(n_x):
            core_copy(q, d, everything, 0).wait_send()
        for d in range(1, n_x):
            x_copy(q, d, everything, 0).wait_send()
        whole = pl.ds(q * seg, seg)
        for e in range(1, n_y):
            remote(
                got_y.at[q, e - 1], got_y.at[q, e - 1], y_send.at[q, e - 1], y_recv.at[q, e - 1, 0], y_device(e)
            ).wait_send()
            remote(
                total.at[whole], got_all.at[q, e - 1], all_send.at[q, e - 1], all_recv.at[q, e - 1, 0], y_device(e)
            ).wait_send()

        @pl.when(z < n_z - 1)
        def _():
            remote(mid.at[whole], up.at[whole], z_send.at[q, 0], z_recv.at[q, 0, 0], (r + n_y, c)).wait_send()

        @pl.when(z > 0)
        def _():
            remote(mid.at[whole], down.at[whole], z_send.at[q, 1], z_recv.at[q, 1, 0], (r - n_y, c)).wait_send()


def shards(rhs, block_target, pivot_inverse, update_factor, root_inverse, update_map):
    n_row, n_col = lax.axis_size("row"), lax.axis_size("col")
    n_y = max(1, n_col // 2)
    n_x = n_col // 2
    width = rhs.shape[1]
    held = rhs.shape[0] // BLK
    rows = pivot_inverse.shape[0]
    parts = width // HALF_LANES
    seg = n_row // n_y // 2 * BLK
    steps = seg // min(EARLY_ROWS, LAST_ROWS)
    f32, bf16 = jnp.float32, jnp.bfloat16
    near = list(range(n_row // 2 - 1, 1, -1))
    cross = list(range(n_row - 1, n_row // 2 - 1, -1))
    order = []
    for n in range(max(len(near), len(cross))):
        order += near[n : n + 1] + cross[n : n + 1]
    order += [1]
    dma = pltpu.SemaphoreType.DMA
    line = pltpu.VMEM((parts * seg, LANES), f32)
    square = pltpu.VMEM((rows, rows), bf16)
    return pl.pallas_call(
        functools.partial(forward_kernel, n_row, n_col, order),
        out_shape=(
            jax.ShapeDtypeStruct((rows, width), f32),
            jax.ShapeDtypeStruct((BLK, width), f32),
        ),
        in_specs=[SMEM, SMEM, VMEM, ANY, ANY, ANY],
        out_specs=(VMEM, VMEM),
        scratch_shapes=[
            pltpu.VMEM((parts, n_row - 1, BLK, LANES), f32),
            pltpu.VMEM((n_row - 1, 8, 128), jnp.int32),
            pltpu.VMEM((n_row, 8, 128), jnp.int32),
            pltpu.SMEM((n_row, 8, 128), jnp.int32),
            pltpu.SMEM((held,), jnp.int32),
            pltpu.VMEM((2 * rows, rows), f32),
        ]
        + [square] * 4
        + [
            pltpu.VMEM((rows, LANES), bf16),
            pltpu.VMEM((rows, LANES), bf16),
            pltpu.VMEM((rows // BLK, BLK, LANES), f32),
            pltpu.VMEM((parts, n_x, n_y * seg, LANES), f32),
            pltpu.VMEM((parts, n_x, n_y * seg, LANES), f32),
            pltpu.VMEM((parts, n_x - 1, n_y * seg, LANES), f32),
            pltpu.VMEM((parts, n_y - 1, seg, LANES), f32),
        ]
        + [line] * 5
        + [
            pltpu.VMEM((parts, n_y - 1, seg, LANES), f32),
            pltpu.VMEM((parts, n_col, BLK // 2, LANES), f32),
            pltpu.VMEM((parts, n_col - 1, BLK // 2, LANES), f32),
            dma((max(2, n_y),)),
            dma(()),
        ]
        + [dma((parts, n_row - 1))] * 2
        + [dma((n_row - 1,))] * 2
        + [
            dma((parts, n_x)),
            dma((parts, n_x, steps)),
            dma((parts, n_x - 1)),
            dma((parts, n_x - 1, steps)),
            dma((parts, n_y - 1)),
            dma((parts, n_y - 1, steps)),
            dma((parts, 2)),
            dma((parts, 2, steps)),
            dma((parts, n_y - 1)),
            dma((parts, n_y - 1, steps)),
            dma((parts, n_col - 1)),
            dma((parts, n_col - 1)),
        ]
        + [pltpu.VMEM((n_row, BLK, LANES), f32)] * parts,
        compiler_params=pltpu.CompilerParams(
            collective_id=0, has_side_effects=True, vmem_limit_bytes=67043328
        ),
        name="forward",
    )(block_target, update_map, rhs.reshape(held, BLK, width), pivot_inverse, update_factor, root_inverse)


def solution(mesh):
    return jax.shard_map(
        shards,
        mesh=mesh,
        in_specs=(
            P(("row", "col"), None),
            P(("row", "col")),
            P(("row", "col"), None),
            P(("row", "col"), None),
            P("row", "col"),
            P(("row", "col")),
        ),
        out_specs=(P(("row", "col"), None), P(("row", "col"), None)),
        check_vma=False,
    )
```

time: 110 us -> 108 us (0.982)
    pallas_call x1, Pallas kernels: 104 us -> 103 us  [shards(): pl.pallas_call(functools.partial(forward_kernel, n_row, n_col, order), ou...]
where the time goes in v1:
time: 108 us
  Pallas kernels  103 us (95%)
  local copies, waits for them, and re-layouts  3.83 us (4%)
    pallas_call x1, Pallas kernels, shards(): pl.pallas_call(functools.partial(forward_kernel, n_row, n_col, order), ou...  103 us
    unnamed x2, local copies, waits for them, and re-layouts  3.83 us

profile of v1, /device:TPU:0, one launch (start us, length us, event | category | flops | bytes accessed | tf_op | source)
XLA Modules:
  0.0 107.7 jit_solution(18098035060933348570)
XLA Ops:
  0.6 103.2 %forward.1 = (f32[1024,256]{1,0:T(8,128)}, f32[128,256]{1,0:T(8,128)}) custom-call(s32[16]{0:T(128)} %target_ref.1, s32[8]{0:T(128)} %map_ref.1, f32[16,128,256]{2,1,0:T(8,128)} %bitcast.1, f32[1024,1024]{1,0:T(8,128)} %pivot_hbm.1, f32[1024,1024]{1,0:T(8,128)} %factor_hbm.1, f32[512,1024]{1,0:T(8,128)} %inverse_hbm.1), custom_call_target="tpu_custom_call" | custom-call | tf_op jit(solution)/shard_map/forward/pallas_call | solution.py:479
  103.9 2.3 %copy.10 = f32[1024,256]{1,0:T(8,128)} copy(f32[1024,256]{1,0:T(8,128)} %get-tuple-element.4) | data formatting | bytes 2097152
  106.1 1.6 %copy.11 = f32[128,256]{1,0:T(8,128)} copy(f32[128,256]{1,0:T(8,128)} %get-tuple-element.5) | data formatting | bytes 262144

commit v2 on v1

--- a/solution.py
+++ b/solution.py
@@ -1,4 +1,6 @@
 import functools
+AHEAD = 2
+AFTER = 1
 import jax
 import jax.numpy as jnp
 from jax import lax
@@ -130,14 +132,19 @@
             pl.semaphore_wait(barrier, n_row + n_col - 2)
         slot_copy(n, d).start()
         data_copy(n, d, 0).start()
-    for n, d in enumerate(order):
-        data_copy(n, d, 1).start()
+
+    def issue(q):
+        if q < parts:
+            for n, d in enumerate(order):
+                data_copy(n, d, q).start()
+
+    for q in range(1, min(2, AHEAD)):
+        issue(q)
     for tile in range(1, parts // 2):
         for n, d in enumerate(order):
             staging[2 * tile, n], staging[2 * tile + 1, n] = stage(*picks[n], tile)
-        for q in (2 * tile, 2 * tile + 1):
-            for n, d in enumerate(order):
-                data_copy(n, d, q).start()
+    for q in range(2, AHEAD):
+        issue(q)
     first, second, slots[r] = chosen(r)
     for tile in range(parts // 2):
         arrived[2 * tile][r], arrived[2 * tile + 1][r] = stage(first, second, tile)
@@ -392,11 +399,14 @@
         stages = [
             (0, steps[q], of(stage_core, q)),
             (1, steps[q], of(stage_x, q)),
-            (3, steps[q], of(stage_y, q)),
         ]
         if q:
-            stages.append((0, steps[q - 1], of(z_first, q - 1)))
+            stages.append((0, steps[q - 1], of(stage_y, q - 1)))
+        if q > 1:
+            stages.append((0, steps[q - 2], of(z_first, q - 2)))
+        if AFTER == 0: issue(q + AHEAD)
         run(stages)
+        if AFTER == 1: issue(q + AHEAD)
         if q % 2:
             solve(q - 1)
 
@@ -409,7 +419,9 @@
         (CORE_SKEW, steps[last], of(stage_x, last)),
         (CORE_SKEW + LEAD, steps[last], of(stage_y, last)),
         (at, steps[last], of(z_first, last)),
-        (0, steps[last - 1], of(z_first, last - 1)),
+        (0, steps[last - 1], of(stage_y, last - 1)),
+        (0, steps[last - 2], of(z_first, last - 2)),
+        (4, steps[last - 1], of(z_first, last - 1)),
         (2, 1, lambda i: solve(last - 1)),
     ]
     for step in range(1, n_z - 1):

time: 108 us -> 96.1 us (0.89)
  Pallas kernels: 103 us -> 91.4 us
    pallas_call x1, Pallas kernels: 103 us -> 91.4 us  [shards(): pl.pallas_call(functools.partial(forward_kernel, n_row, n_col, order), ou...]
where the time goes in v2:
time: 96.1 us; the launch traced here: 95.9 us
  Pallas kernels  91.4 us (95%)
  local copies, waits for them, and re-layouts  3.83 us (4%)
    pallas_call x1, Pallas kernels, shards(): pl.pallas_call(functools.partial(forward_kernel, n_row, n_col, order), ou...  91.4 us
    unnamed x2, local copies, waits for them, and re-layouts  3.83 us

profile of v2, /device:TPU:0, one launch (start us, length us, event | category | flops | bytes accessed | tf_op | source)
XLA Modules:
  0.0 95.9 jit_solution(2910776043382511447)
XLA Ops:
  0.6 91.4 %forward.1 = (f32[1024,256]{1,0:T(8,128)}, f32[128,256]{1,0:T(8,128)}) custom-call(s32[16]{0:T(128)} %target_ref.1, s32[8]{0:T(128)} %map_ref.1, f32[16,128,256]{2,1,0:T(8,128)} %bitcast.1, f32[1024,1024]{1,0:T(8,128)} %pivot_hbm.1, f32[1024,1024]{1,0:T(8,128)} %factor_hbm.1, f32[512,1024]{1,0:T(8,128)} %inverse_hbm.1), custom_call_target="tpu_custom_call" | custom-call | tf_op jit(solution)/shard_map/forward/pallas_call | solution.py:491
  92.1 2.3 %copy.10 = f32[1024,256]{1,0:T(8,128)} copy(f32[1024,256]{1,0:T(8,128)} %get-tuple-element.4) | data formatting | bytes 2097152
  94.3 1.6 %copy.11 = f32[128,256]{1,0:T(8,128)} copy(f32[128,256]{1,0:T(8,128)} %get-tuple-element.5) | data formatting | bytes 262144

commit v3 on v1

--- a/solution.py
+++ b/solution.py
@@ -11,12 +11,17 @@
 LANES = 128
 HALF_LANES = 64
 TILE = 256
-EARLY_ROWS = 64
+EARLY_ROWS = 128
 LAST_ROWS = 32
-CORE_SKEW = 2
+WINDOW = 4
+CORE_SKEW = 1
 LEAD = 4
 SKEW = 3
-Z_SKEW = 4
+EARLY_HOPS = 0
+SOLVE = 12
+LATE = True
+OLD = (0, 2, 5)
+OLD_SKEW = 4
 MESH = pl.DeviceIdType.MESH
 VMEM = pl.BlockSpec(memory_space=pltpu.VMEM)
 SMEM = pl.BlockSpec(memory_space=pltpu.SMEM)
@@ -47,13 +52,13 @@
 
 
 def forward_kernel(
-    n_row, n_col, order, target_ref, map_ref, rhs_ref, pivot_hbm, factor_hbm, inverse_hbm,
-    solved, out,
-    staging, messages, slots, slots_smem, place_ref, weights,
+    n_row, n_col, order, target_ref, map_ref, rhs_hbm, pivot_hbm, factor_hbm, inverse_hbm,
+    solved_hbm, out,
+    rhs_ref, solved, staging, messages, slots, slots_smem, place_ref, weights,
     p_high, p_low, w_high, w_low, x_high, x_low, updated,
-    give, got_core, got_x, got_y, mid, up, down, ds, total, got_all, product, got_col,
-    weight_sem, slot_sem, send, recv, send_int, recv_int,
-    core_send, core_recv, x_send, x_recv, y_send, y_recv, z_send, z_recv, all_send, all_recv,
+    give, got_core, got_x, got_y, got_near, mid, up, down, ds, total, got_all, product, got_col,
+    weight_sem, rhs_sem, solved_sem, slot_sem, send, recv, send_int, recv_int,
+    core_send, core_recv, x_send, x_recv, y_send, y_recv, near_send, near_recv, z_send, z_recv, all_send, all_recv,
     col_send, col_recv, *arrived,
 ):
     n_y = max(1, n_col // 2)
@@ -83,11 +88,23 @@
             src_ref=src, dst_ref=dst, send_sem=ss, recv_sem=rs, device_id=device, device_id_type=MESH
         )
 
+    rhs_copy = pltpu.make_async_copy(rhs_hbm, rhs_ref, rhs_sem)
+    rhs_copy.start()
+
+    def near_device(d, e):
+        return (r - y + (y + e) % n_y, (x + d) % n_x * 2 + k)
+
+    near = [(d, e) for d in range(n_x - 1, -1, -1) for e in range(n_y - 1, -1, -1) if d or e]
+    diagonal = [(d, e) for d, e in near if d and e]
+
     barrier = pltpu.get_barrier_semaphore()
     for d in order:
         pl.semaphore_signal(barrier, inc=1, device_id=(r ^ d, c), device_id_type=MESH)
     for d in range(1, n_col):
         pl.semaphore_signal(barrier, inc=1, device_id=(r, (c + d) % n_col), device_id_type=MESH)
+
+    for d, e in diagonal:
+        pl.semaphore_signal(barrier, inc=1, device_id=near_device(d, e), device_id_type=MESH)
 
     pivot_copy = pltpu.make_async_copy(pivot_hbm, weights.at[pl.ds(0, rows)], weight_sem.at[0])
     factor_copy = pltpu.make_async_copy(factor_hbm, weights.at[pl.ds(rows, rows)], weight_sem.at[1])
@@ -121,23 +138,27 @@
     def slot_copy(n, d):
         return remote(messages.at[n], slots.at[r], send_int.at[n], recv_int.at[n], (r ^ d, c))
 
+    rhs_copy.wait()
     picks = []
     for n, d in enumerate(order):
         first, second, messages[n] = chosen(r ^ d)
         picks.append((first, second))
         staging[0, n], staging[1, n] = stage(first, second, 0)
         if n == 0:
-            pl.semaphore_wait(barrier, n_row + n_col - 2)
+            pl.semaphore_wait(barrier, n_row + n_col - 2 + len(diagonal))
         slot_copy(n, d).start()
         data_copy(n, d, 0).start()
-    for n, d in enumerate(order):
-        data_copy(n, d, 1).start()
     for tile in range(1, parts // 2):
         for n, d in enumerate(order):
             staging[2 * tile, n], staging[2 * tile + 1, n] = stage(*picks[n], tile)
-        for q in (2 * tile, 2 * tile + 1):
-            for n, d in enumerate(order):
-                data_copy(n, d, q).start()
+    queue = [(n, d, q) for q in range(1, parts) for n, d in enumerate(order)]
+
+    def pump(n, d, q):
+        data_copy(n, d, q).wait_recv()
+        reached = q * len(order) + n + WINDOW
+        while queue and queue[0][2] * len(order) + queue[0][0] <= reached:
+            data_copy(*queue.pop(0)).start()
+
     first, second, slots[r] = chosen(r)
     for tile in range(parts // 2):
         arrived[2 * tile][r], arrived[2 * tile + 1][r] = stage(first, second, tile)
@@ -193,8 +214,6 @@
         return jnp.where(side == lax.rem(place, CAP), value, swap(value))
 
     def update(q):
-        for n, d in enumerate(order):
-            data_copy(n, d, q).wait_recv()
         for b in range(half):
             part = slice(b * BLK, (b + 1) * BLK)
             x_high[part], x_low[part] = split(twice(q, b))
@@ -214,6 +233,10 @@
             solved[band, q // 2 * LANES : (q // 2 + 1) * LANES] = dot3(
                 p_high[band, deep], p_low[band, deep], x_high[deep], x_low[deep]
             )
+
+    def keep(q):
+        cols = pl.ds(q // 2 * LANES, LANES)
+        return pltpu.make_async_copy(solved.at[:, cols], solved_hbm.at[:, cols], solved_sem.at[q // 2])
 
     def within(q, i):
         return pl.ds(pl.multiple_of(i * chunk[q], chunk[q]), chunk[q])
@@ -240,24 +263,31 @@
             give.at[q, d, part], got_core.at[q, d, part], core_send.at[q, d], core_recv.at[q, d, i], partner
         )
 
+    def y_device(e):
+        return (r - y + (y + e) % n_y, c)
+
+    def slab(q, i, e):
+        return pl.ds(pl.multiple_of((i * n_y + e) * chunk[q], chunk[q]), chunk[q])
+
     def x_copy(q, d, part, i):
         return remote(
             got_core.at[q, d, part], got_x.at[q, d - 1, part], x_send.at[q, d - 1], x_recv.at[q, d - 1, i],
             (r, (x + d) % n_x * 2 + k),
         )
 
-    def y_device(e):
-        return (r - y + (y + e) % n_y, c)
-
-    def slab(q, i, e):
-        return pl.ds(pl.multiple_of((i * n_y + e) * chunk[q], chunk[q]), chunk[q])
-
     def y_copy(q, e, i):
         return remote(
             got_core.at[q, 0, slab(q, i, e)], got_y.at[q, e - 1, within(q, i)],
             y_send.at[q, e - 1], y_recv.at[q, e - 1, i], y_device(e),
         )
 
+    def near_copy(q, d, e, i):
+        at = d * n_y + e - 1
+        return remote(
+            got_core.at[q, d, slab(q, i, e)], got_near.at[at, within(q, i)],
+            near_send.at[at], near_recv.at[at, i], near_device(d, e),
+        )
+
     def all_copy(q, e, i):
         return remote(
             total.at[place_of(q, i)], got_all.at[q, e - 1, within(q, i)],
@@ -277,6 +307,19 @@
             for e in range(n_y - 1, -1, -1):
                 give[q, d, slab(q, i, e)] = dense(q, 2 * ((x + d) % n_x) + (1 - k), i, e)
             core_copy(q, d, wide(q, i), i).start()
+
+    def stage_near(q, i):
+        for d in range(n_x - 1, -1, -1):
+            values = [dense(q, 2 * ((x + d) % n_x) + k, i, e) for e in range(n_y)]
+            core_copy(q, d, wide(q, i), i).wait_recv()
+            for e in range(n_y - 1, -1, -1):
+                part = slab(q, i, e)
+                value = values[e] + got_core[q, d, part]
+                if d or e:
+                    got_core[q, d, part] = value
+                    near_copy(q, d, e, i).start()
+                else:
+                    mid[place_of(q, i)] = value
 
     def stage_x(q, i):
         for d in range(n_x - 1, -1, -1):
@@ -318,9 +361,14 @@
     def z_first(q, i):
         part = place_of(q, i)
         value = mid[part]
-        for e in range(1, n_y):
-            y_copy(q, e, i).wait_recv()
-            value = value + got_y[q, e - 1, within(q, i)]
+        if q == last:
+            for d, e in reversed(near):
+                near_copy(q, d, e, i).wait_recv()
+                value = value + got_near[d * n_y + e - 1, within(q, i)]
+        else:
+            for e in range(1, n_y):
+                y_copy(q, e, i).wait_recv()
+                value = value + got_y[q, e - 1, within(q, i)]
         mid[part] = value
         hop(0, q, i)
 
@@ -387,45 +435,65 @@
     def of(fn, *args):
         return functools.partial(fn, *args)
 
+    def each(fn, *args):
+        for i in range(steps[args[-1]]):
+            fn(*args, i)
+
+    turns = len(order)
+    for n, d in enumerate(order):
+        pump(n, d, 0)
     for q in range(last):
         update(q)
-        stages = [
-            (0, steps[q], of(stage_core, q)),
-            (1, steps[q], of(stage_x, q)),
-            (3, steps[q], of(stage_y, q)),
-        ]
-        if q:
-            stages.append((0, steps[q - 1], of(z_first, q - 1)))
-        run(stages)
-        if q % 2:
-            solve(q - 1)
-
-    for copy in inverse_copies:
-        copy.wait()
+        for n, d in enumerate(order):
+            if n == 0:
+                each(stage_core, q)
+            if n == 1:
+                each(stage_x, q)
+            if n == 2 and q % 2:
+                solve(q - 1)
+                keep(q - 1).start()
+            if n == 2 and q:
+                each(z_first, q - 1)
+            if n == turns - 2:
+                each(stage_y, q)
+                if q == last - 1:
+                    for copy in inverse_copies:
+                        copy.wait()
+                    for old in range(EARLY_HOPS):
+                        each(hop, 1, old)
+            pump(n, d, q + 1)
+
     update(last)
-    at = CORE_SKEW + LEAD + SKEW
+    count = steps[last]
+    at = CORE_SKEW + LEAD
     stages = [
-        (0, steps[last], of(stage_core, last)),
-        (CORE_SKEW, steps[last], of(stage_x, last)),
-        (CORE_SKEW + LEAD, steps[last], of(stage_y, last)),
-        (at, steps[last], of(z_first, last)),
-        (0, steps[last - 1], of(z_first, last - 1)),
-        (2, 1, lambda i: solve(last - 1)),
+        (0, count, of(stage_core, last)),
+        (CORE_SKEW, count, of(stage_near, last)),
+        (at, count, of(z_first, last)),
     ]
     for step in range(1, n_z - 1):
-        stages.append((at + step * SKEW, steps[last], of(hop, step, last)))
-    stages.append((at + (n_z - 1) * SKEW, steps[last], of(z_last, last)))
+        stages.append((at + step * SKEW, count, of(hop, step, last)))
+    stages.append((at + (n_z - 1) * SKEW, count, of(z_last, last)))
+    stages.append((SOLVE, 1, lambda i: solve(last - 1)))
+    stages.append((0, steps[last - 1], of(z_first, last - 1)))
     for q in range(last):
-        begin = sum(steps[:q])
+        begin = OLD[q]
         for step in range(1, n_z - 1):
-            stages.append((begin + (step - 1) * Z_SKEW, steps[q], of(hop, step, q)))
-        stages.append((begin + (n_z - 2) * Z_SKEW, steps[q], of(z_last, q)))
+            if step > 1 or q >= EARLY_HOPS:
+                stages.append((begin + (step - 1) * OLD_SKEW, steps[q], of(hop, step, q)))
+        stages.append((begin + (n_z - 2) * OLD_SKEW, steps[q], of(z_last, q)))
+        if not LATE:
+            stages.append((begin + (n_z - 1) * OLD_SKEW + 1, 1, functools.partial(lambda q, i: multiply(q), q)))
     run(stages)
-    for q in range(parts):
+    keep(last - 1).start()
+    for q in range(last if LATE else 0):
         multiply(q)
+    multiply(last)
     for q in range(0, parts, 2):
         collect(q)
 
+    for q in range(0, parts, 2):
+        keep(q).wait()
     for n, d in enumerate(order):
         slot_copy(n, d).wait_send()
         for q in range(parts):
@@ -436,13 +504,21 @@
         everything = pl.ds(0, n_y * seg)
         for d in range(n_x):
             core_copy(q, d, everything, 0).wait_send()
-        for d in range(1, n_x):
-            x_copy(q, d, everything, 0).wait_send()
         whole = pl.ds(q * seg, seg)
+        if q == last:
+            for d, e in near:
+                at = d * n_y + e - 1
+                remote(
+                    got_near.at[at], got_near.at[at], near_send.at[at], near_recv.at[at, 0], near_device(d, e)
+                ).wait_send()
+        else:
+            for d in range(1, n_x):
+                x_copy(q, d, everything, 0).wait_send()
+            for e in range(1, n_y):
+                remote(
+                    got_y.at[q, e - 1], got_y.at[q, e - 1], y_send.at[q, e - 1], y_recv.at[q, e - 1, 0], y_device(e)
+                ).wait_send()
         for e in range(1, n_y):
-            remote(
-                got_y.at[q, e - 1], got_y.at[q, e - 1], y_send.at[q, e - 1], y_recv.at[q, e - 1, 0], y_device(e)
-            ).wait_send()
             remote(
                 total.at[whole], got_all.at[q, e - 1], all_send.at[q, e - 1], all_recv.at[q, e - 1, 0], y_device(e)
             ).wait_send()
@@ -482,9 +558,11 @@
             jax.ShapeDtypeStruct((rows, width), f32),
             jax.ShapeDtypeStruct((BLK, width), f32),
         ),
-        in_specs=[SMEM, SMEM, VMEM, ANY, ANY, ANY],
-        out_specs=(VMEM, VMEM),
+        in_specs=[SMEM, SMEM, ANY, ANY, ANY, ANY],
+        out_specs=(ANY, VMEM),
         scratch_shapes=[
+            pltpu.VMEM((held, BLK, width), f32),
+            pltpu.VMEM((rows, width), f32),
             pltpu.VMEM((parts, n_row - 1, BLK, LANES), f32),
             pltpu.VMEM((n_row - 1, 8, 128), jnp.int32),
             pltpu.VMEM((n_row, 8, 128), jnp.int32),
@@ -499,8 +577,9 @@
             pltpu.VMEM((rows // BLK, BLK, LANES), f32),
             pltpu.VMEM((parts, n_x, n_y * seg, LANES), f32),
             pltpu.VMEM((parts, n_x, n_y * seg, LANES), f32),
-            pltpu.VMEM((parts, n_x - 1, n_y * seg, LANES), f32),
-            pltpu.VMEM((parts, n_y - 1, seg, LANES), f32),
+            pltpu.VMEM((parts - 1, n_x - 1, n_y * seg, LANES), f32),
+            pltpu.VMEM((parts - 1, n_y - 1, seg, LANES), f32),
+            pltpu.VMEM((n_x * n_y - 1, seg, LANES), f32),
         ]
         + [line] * 5
         + [
@@ -509,16 +588,20 @@
             pltpu.VMEM((parts, n_col - 1, BLK // 2, LANES), f32),
             dma((max(2, n_y),)),
             dma(()),
+            dma((parts // 2,)),
+            dma(()),
         ]
         + [dma((parts, n_row - 1))] * 2
         + [dma((n_row - 1,))] * 2
         + [
             dma((parts, n_x)),
             dma((parts, n_x, steps)),
-            dma((parts, n_x - 1)),
-            dma((parts, n_x - 1, steps)),
-            dma((parts, n_y - 1)),
-            dma((parts, n_y - 1, steps)),
+            dma((parts - 1, n_x - 1)),
+            dma((parts - 1, n_x - 1, steps)),
+            dma((parts - 1, n_y - 1)),
+            dma((parts - 1, n_y - 1, steps)),
+            dma((n_x * n_y - 1,)),
+            dma((n_x * n_y - 1, steps)),
             dma((parts, 2)),
             dma((parts, 2, steps)),
             dma((parts, n_y - 1)),

time: 108 us -> 92.6 us (0.86)
  Pallas kernels: 103 us -> 87.9 us
    pallas_call x1, Pallas kernels: 103 us -> 87.9 us  [shards(): pl.pallas_call(functools.partial(forward_kernel, n_row, n_col, order), ou...]
where the time goes in v3:
time: 92.6 us; the launch traced here: 92.4 us
  Pallas kernels  87.9 us (95%)
  local copies, waits for them, and re-layouts  3.83 us (4%)
    pallas_call x1, Pallas kernels, shards(): pl.pallas_call(functools.partial(forward_kernel, n_row, n_col, order), ou...  87.9 us
    unnamed x2, local copies, waits for them, and re-layouts  3.83 us

profile of v3, /device:TPU:0, one launch (start us, length us, event | category | flops | bytes accessed | tf_op | source)
XLA Modules:
  0.0 92.4 jit_solution(3936102520506249200)
XLA Ops:
  0.6 87.9 %forward.1 = (f32[1024,256]{1,0:T(8,128)}, f32[128,256]{1,0:T(8,128)}) custom-call(s32[16]{0:T(128)} %target_ref.1, s32[8]{0:T(128)} %map_ref.1, f32[16,128,256]{2,1,0:T(8,128)} %bitcast.1, f32[1024,1024]{1,0:T(8,128)} %pivot_hbm.1, f32[1024,1024]{1,0:T(8,128)} %factor_hbm.1, f32[512,1024]{1,0:T(8,128)} %inverse_hbm.1), custom_call_target="tpu_custom_call" | custom-call | tf_op jit(solution)/shard_map/forward/pallas_call | solution.py:555
  88.5 2.3 %copy.10 = f32[1024,256]{1,0:T(8,128)} copy(f32[1024,256]{1,0:T(8,128)} %get-tuple-element.4) | data formatting | bytes 2097152
  90.8 1.6 %copy.11 = f32[128,256]{1,0:T(8,128)} copy(f32[128,256]{1,0:T(8,128)} %get-tuple-element.5) | data formatting | bytes 262144

commit v4 on v3

--- a/solution.py
+++ b/solution.py
@@ -19,7 +19,6 @@
 SKEW = 3
 EARLY_HOPS = 0
 SOLVE = 12
-LATE = True
 OLD = (0, 2, 5)
 OLD_SKEW = 4
 MESH = pl.DeviceIdType.MESH
@@ -482,11 +481,11 @@
             if step > 1 or q >= EARLY_HOPS:
                 stages.append((begin + (step - 1) * OLD_SKEW, steps[q], of(hop, step, q)))
         stages.append((begin + (n_z - 2) * OLD_SKEW, steps[q], of(z_last, q)))
-        if not LATE:
-            stages.append((begin + (n_z - 1) * OLD_SKEW + 1, 1, functools.partial(lambda q, i: multiply(q), q)))
+        if q < last - 1:
+            stages.append((14 + 2 * q, 1, functools.partial(lambda q, i: multiply(q), q)))
     run(stages)
     keep(last - 1).start()
-    for q in range(last if LATE else 0):
+    for q in range(last - 1, last):
         multiply(q)
     multiply(last)
     for q in range(0, parts, 2):
@@ -532,6 +531,17 @@
             remote(mid.at[whole], down.at[whole], z_send.at[q, 1], z_recv.at[q, 1, 0], (r - n_y, c)).wait_send()
 
 
+def place_kernel(solved, root, solved_out, root_out, sem):
+    copies = [
+        pltpu.make_async_copy(solved, solved_out, sem.at[0]),
+        pltpu.make_async_copy(root, root_out, sem.at[1]),
+    ]
+    for copy in copies:
+        copy.start()
+    for copy in copies:
+        copy.wait()
+
+
 def shards(rhs, block_target, pivot_inverse, update_factor, root_inverse, update_map):
     n_row, n_col = lax.axis_size("row"), lax.axis_size("col")
     n_y = max(1, n_col // 2)
@@ -552,7 +562,7 @@
     dma = pltpu.SemaphoreType.DMA
     line = pltpu.VMEM((parts * seg, LANES), f32)
     square = pltpu.VMEM((rows, rows), bf16)
-    return pl.pallas_call(
+    results = pl.pallas_call(
         functools.partial(forward_kernel, n_row, n_col, order),
         out_shape=(
             jax.ShapeDtypeStruct((rows, width), f32),
@@ -615,6 +625,14 @@
         ),
         name="forward",
     )(block_target, update_map, rhs.reshape(held, BLK, width), pivot_inverse, update_factor, root_inverse)
+    return pl.pallas_call(
+        place_kernel,
+        out_shape=tuple(jax.ShapeDtypeStruct(result.shape, f32) for result in results),
+        in_specs=[VMEM, VMEM],
+        out_specs=(ANY, ANY),
+        scratch_shapes=[dma((2,))],
+        name="place",
+    )(*results)
 
 
 def solution(mesh):

time: 92.6 us -> 90.5 us (0.977)
  local copies, waits for them, and re-layouts: 3.83 us -> 0 us
  Pallas kernels: 87.9 us -> 89.5 us
    unnamed x2 -> x0, local copies, waits for them, and re-layouts: 3.83 us -> none
    pallas_call x0 -> x1, Pallas kernels: none -> 2.24 us  [shards(): pl.pallas_call(place_kernel, out_shape=tuple((jax.ShapeDtypeStruct(result...]
where the time goes in v4:
time: 90.5 us; the launch traced here: 90.3 us
  Pallas kernels  89.5 us (99%)
    pallas_call x1, Pallas kernels, shards(): pl.pallas_call(functools.partial(forward_kernel, n_row, n_col, order), ou...  87.3 us
    pallas_call x1, Pallas kernels, shards(): pl.pallas_call(place_kernel, out_shape=tuple((jax.ShapeDtypeStruct(result...  2.24 us

profile of v4, /device:TPU:0, one launch (start us, length us, event | category | flops | bytes accessed | tf_op | source)
XLA Modules:
  0.0 90.3 jit_solution(17735920818844620260)
XLA Ops:
  0.6 87.3 %forward.1 = (f32[1024,256]{1,0:T(8,128)}, f32[128,256]{1,0:T(8,128)}) custom-call(s32[16]{0:T(128)} %target_ref.1, s32[8]{0:T(128)} %map_ref.1, f32[16,128,256]{2,1,0:T(8,128)} %bitcast.1, f32[1024,1024]{1,0:T(8,128)} %pivot_hbm.1, f32[1024,1024]{1,0:T(8,128)} %factor_hbm.1, f32[512,1024]{1,0:T(8,128)} %inverse_hbm.1), custom_call_target="tpu_custom_call" | custom-call | tf_op jit(solution)/shard_map/forward/pallas_call | solution.py:565
  87.9 2.2 %place.1 = (f32[1024,256]{1,0:T(8,128)}, f32[128,256]{1,0:T(8,128)}) custom-call(f32[1024,256]{1,0:T(8,128)} %get-tuple-element.4.solved, f32[128,256]{1,0:T(8,128)} %get-tuple-element.5.root), custom_call_target="tpu_custom_call" | custom-call | tf_op jit(solution)/shard_map/place/pallas_call | solution.py:628

commit v5 on v4

--- a/solution.py
+++ b/solution.py
@@ -11,7 +11,7 @@
 LANES = 128
 HALF_LANES = 64
 TILE = 256
-EARLY_ROWS = 128
+EARLY_ROWS = 64
 LAST_ROWS = 32
 WINDOW = 4
 CORE_SKEW = 1

time: 90.5 us -> 90.6 us (level)
  no operation moved by 1% of the time
where the time goes in v5:
time: 90.6 us; the launch traced here: 90.4 us
  Pallas kernels  89.6 us (99%)
    pallas_call x1, Pallas kernels, shards(): pl.pallas_call(functools.partial(forward_kernel, n_row, n_col, order), ou...  87.4 us
    pallas_call x1, Pallas kernels, shards(): pl.pallas_call(place_kernel, out_shape=tuple((jax.ShapeDtypeStruct(result...  2.24 us

profile of v5, /device:TPU:0, one launch (start us, length us, event | category | flops | bytes accessed | tf_op | source)
XLA Modules:
  0.0 90.4 jit_solution(10035244760593758700)
XLA Ops:
  0.6 87.4 %forward.1 = (f32[1024,256]{1,0:T(8,128)}, f32[128,256]{1,0:T(8,128)}) custom-call(s32[16]{0:T(128)} %target_ref.1, s32[8]{0:T(128)} %map_ref.1, f32[16,128,256]{2,1,0:T(8,128)} %bitcast.1, f32[1024,1024]{1,0:T(8,128)} %pivot_hbm.1, f32[1024,1024]{1,0:T(8,128)} %factor_hbm.1, f32[512,1024]{1,0:T(8,128)} %inverse_hbm.1), custom_call_target="tpu_custom_call" | custom-call | tf_op jit(solution)/shard_map/forward/pallas_call | solution.py:565
  88.0 2.2 %place.1 = (f32[1024,256]{1,0:T(8,128)}, f32[128,256]{1,0:T(8,128)}) custom-call(f32[1024,256]{1,0:T(8,128)} %get-tuple-element.4.solved, f32[128,256]{1,0:T(8,128)} %get-tuple-element.5.root), custom_call_target="tpu_custom_call" | custom-call | tf_op jit(solution)/shard_map/place/pallas_call | solution.py:628
